TPU v7x, 32 devices: a whole 2x2x4 slice. The times are simulated.
32 devices in a mesh: ctx: 8 (over z, x), tp: 4 (over y, core).
Axes of the slice: x: 2, y: 2, z: 4, core: 2. Of those that a mesh axis runs over, the one named last changes fastest.
Arguments:
- queries: bfloat16 [64, 4, 64, 128], P('ctx', None, 'tp'), may hold values from -250 to 250
- new_keys: bfloat16 [64, 4, 8, 128], P('ctx', None, 'tp'), may hold values from -6 to 6
- new_values: bfloat16 [64, 4, 8, 128], P('ctx', None, 'tp'), may hold values from -24 to 24
- key_pool: bfloat16 [512, 256, 8, 128], P('ctx', None, 'tp'), may hold values from -6 to 6
- value_pool: bfloat16 [512, 256, 8, 128], P('ctx', None, 'tp'), may hold values from -24 to 24
- slot_block: int32 [512], P('ctx'), may hold values from -1 to 8191, as said below
- lengths: int32 [64], replicated, may hold values from 1 to 32768, as said below
- out_weight: bfloat16 [8192, 8192], P('tp', 'ctx'), may hold values from -0.0625 to 0.0625
Outputs:
- layer_out: bfloat16 [64, 4, 8192], P('tp', None, 'ctx')
Inputs may be any that keep to these rules, and one draw needn't show every extreme that they name: `slot_block`: each entry is r * 128 + j for block j of request r, or -1 for an empty slot. Every block j < b_r of every request r appears exactly once, where b_r = ceil(lengths[r] / 256). On each index of ctx the used slots come first. The owner of a request holds its first blocks as far as its slots reach; the remaining blocks lie on other indices of ctx. The blocks that one index of ctx holds of requests it does not own all belong to one request, and some index of ctx holds such blocks. `lengths`: some request has exactly 32768 positions.
All inputs are finite; a program needn't handle non-finite values.
Results may differ from a plain program's by a relative error of at most 0.006.
Values may be sent and summed in bfloat16 or wider, within the bound.
No kernel may reach another device: no remote copies, remote signals or barrier semaphores. Data moves between devices by JAX's collectives and lax.ppermute only.
A program may use at most 64 MiB of HBM per device.

v0:
```python
import functools
import math

import jax
import jax.numpy as jnp
from jax import lax
from jax.experimental import pallas as pl
from jax.experimental.pallas import tpu as pltpu
from jax.sharding import PartitionSpec as P


MAXB = 128
GROUP = 8
AHEAD = 32
COST = 10**10
NEG = -1e30
LOG2E = math.log2(math.e)
F32 = jnp.float32
BF16 = jnp.bfloat16

NT = (((1,), (1,)), ((), ()))


def request_kernel(owned, rows, block_len, round_ref, slot_ref, len_ref, q_ref, out_ref, count):
    me = lax.axis_index("ctx")
    for r in range(owned):
        count[r] = 0

    shift = MAXB.bit_length() - 1

    def tally(s, carry):
        local = lax.shift_right_arithmetic(slot_ref[s], shift) - me * owned
        local = jnp.where((local >= 0) & (local < owned), local, owned)
        count[local] = count[local] + 1
        return carry

    lax.fori_loop(0, slot_ref.shape[0], tally, 0, unroll=8)
    seen = jnp.int32(0)
    pick = jnp.int32(-1)
    for r in range(owned):
        blocks = lax.div(len_ref[me * owned + r] + (block_len - 1), block_len)
        lent = count[r] < blocks
        pick = jnp.where(lent & (seen == round_ref[0]), r, pick)
        seen = seen + lent.astype(jnp.int32)
    row = lax.broadcasted_iota(jnp.int32, (16, 128), 0)
    info = jnp.where(row == 0, seen, pick).astype(F32).astype(BF16)
    body = q_ref[jnp.maximum(pick, 0)]
    for c in range(out_ref.shape[0]):
        out_ref[c, pl.ds(0, rows), :] = body
        out_ref[c, pl.ds(rows, 16), :] = info


def attend(
    foreign, owned, kv, group, slot_ref, len_ref, query_of, first,
    k_hbm, v_hbm, kbuf, vbuf, ksem, vsem, order, sbuf, hbuf, m_acc, l_acc, a_acc,
):
    me = lax.axis_index("ctx")
    width, head = kbuf.shape[1:]
    block_len = width // kv
    rows = m_acc.shape[1]
    heads = group * kv
    coef = head ** -0.5 * LOG2E
    shift = MAXB.bit_length() - 1
    low, past = me * owned, (me + 1) * owned

    def begin(s, n):
        code = slot_ref[s]
        r = lax.shift_right_arithmetic(code, shift)
        inside = (r >= low) & (r < past)
        mine = (code >= 0) & (jnp.logical_not(inside) if foreign else inside)
        order[n] = s
        return n + mine.astype(jnp.int32)

    n = lax.fori_loop(0, slot_ref.shape[0], begin, jnp.int32(0), unroll=8)

    def fetch(i, carry):
        s = order[i]
        pltpu.make_async_copy(k_hbm.at[s], kbuf.at[i], ksem.at[i]).start()
        pltpu.make_async_copy(v_hbm.at[s], vbuf.at[i], vsem.at[i]).start()
        return carry

    lax.fori_loop(0, jnp.minimum(n, AHEAD), fetch, 0)
    first()
    col = lax.broadcasted_iota(jnp.int32, (2 * rows, width), 1)
    row = lax.broadcasted_iota(jnp.int32, (2 * rows, width), 0)
    same = (col % kv) == (row % heads) // group
    place = jnp.where(same, col, width * 2)
    none = jnp.zeros((rows, head), BF16)

    def at(i):
        slot = jnp.minimum(i, n - 1)
        code = slot_ref[order[slot]]
        r = lax.shift_right_arithmetic(code, shift)
        valid = jnp.clip(len_ref[r] - (code - r * MAXB) * block_len, 0, block_len)
        valid = jnp.where(i < n, valid, 0) * kv
        return slot, (jnp.int32(0) if foreign else r - low), valid

    def wait(base, source, buf, sem):
        for g in range(GROUP):
            i = base + g

            @pl.when(i < n)
            def _():
                pltpu.make_async_copy(source.at[0], buf.at[i], sem.at[i]).wait()

    def score(base, side):
        for p in range(GROUP // 2):
            sa, ea, va = at(base + 2 * p)
            sb, eb, vb = at(base + 2 * p + 1)
            left = jnp.concatenate(
                [
                    jnp.concatenate([query_of(ea), none], axis=1),
                    jnp.concatenate([none, query_of(eb)], axis=1),
                ],
                axis=0,
            )
            right = jnp.concatenate([kbuf[sa], kbuf[sb]], axis=1)
            raw = lax.dot_general(left, right, NT, preferred_element_type=F32)
            for half, valid in ((0, va), (1, vb)):
                part = slice(half * rows, (half + 1) * rows)
                masked = jnp.where(place[part] < valid, raw[part], NEG)
                sbuf[side, p, part, :] = masked
                high = jnp.max(masked, axis=1, keepdims=True)
                hbuf[side, p, part, :] = jnp.broadcast_to(high, (rows, 128))

    def mix(base, side):
        for p in range(GROUP // 2):
            sa, ea, _ = at(base + 2 * p)
            sb, eb, _ = at(base + 2 * p + 1)
            high = hbuf[side, p]
            total = None
            pieces = []
            for c in range(width // 128):
                w = jnp.exp2((sbuf[side, p, :, c * 128 : (c + 1) * 128] - high) * coef).astype(BF16)
                pieces.append(w)
                rounded = w.astype(F32)
                total = rounded if total is None else total + rounded
            weights = jnp.concatenate(pieces, axis=1)
            right = jnp.concatenate([vbuf[sa], vbuf[sb]], axis=1)
            summed = jnp.dot(weights, right, preferred_element_type=F32)
            for half, e in ((0, ea), (1, eb)):
                part = slice(half * rows, (half + 1) * rows)
                before = m_acc[e]
                peak = jnp.maximum(before, high[part])
                keep = jnp.exp2((before - peak) * coef)
                add = jnp.exp2((high[part] - peak) * coef)
                m_acc[e] = peak
                l_acc[e] = l_acc[e] * keep + total[part] * add
                a_acc[e] = a_acc[e] * keep + summed[part, half * head : (half + 1) * head] * add

    def step(it, carry):
        base = it * GROUP
        lax.fori_loop(jnp.minimum(base + AHEAD, n), jnp.minimum(base + GROUP + AHEAD, n), fetch, 0)
        wait(base + GROUP, k_hbm, kbuf, ksem)
        wait(base, v_hbm, vbuf, vsem)
        side = lax.rem(it, 2)
        score(base + GROUP, 1 - side)
        mix(base, side)
        return carry

    @pl.when(n > 0)
    def _():
        wait(0, k_hbm, kbuf, ksem)
        score(0, 0)
        lax.fori_loop(0, lax.div(n + GROUP - 1, GROUP), step, 0)


def own_kernel(
    owned, steps, kv, group, slot_ref, len_ref, q_ref, nk_hbm, nv_hbm, k_hbm, v_hbm,
    out_ref, lse_ref, nk_ref, nv_ref, nsem, kbuf, vbuf, ksem, vsem, order, sbuf, hbuf, m_acc, l_acc, a_acc,
):
    rows, head = q_ref.shape[1:]
    heads = kv * group
    coef = head ** -0.5 * LOG2E
    fresh = nk_ref.shape[0]
    nk_copy = pltpu.make_async_copy(nk_hbm, nk_ref, nsem.at[0])
    nv_copy = pltpu.make_async_copy(nv_hbm, nv_ref, nsem.at[1])
    nk_copy.start()
    nv_copy.start()
    col = lax.broadcasted_iota(jnp.int32, (rows, fresh), 1)
    row = lax.broadcasted_iota(jnp.int32, (rows, fresh), 0)
    seen = ((col % kv) == (row % heads) // group) & (lax.div(col, kv) % steps <= lax.div(row, heads))
    lane = lax.broadcasted_iota(jnp.int32, (rows, 128), 1)

    def first():
        nk_copy.wait()
        nv_copy.wait()
        nk = nk_ref[...]
        nv = nv_ref[...]
        for r in range(owned):
            scores = lax.dot_general(q_ref[r], nk, NT, preferred_element_type=F32)
            ok = seen & (lax.div(col, kv * steps) == r)
            scores = jnp.where(ok, scores, NEG)
            high = jnp.max(scores, axis=1, keepdims=True)
            weights = jnp.where(ok, jnp.exp2((scores - high) * coef), 0.0).astype(BF16)
            total = jnp.sum(weights.astype(F32), axis=1, keepdims=True)
            m_acc[r] = jnp.broadcast_to(high, (rows, 128))
            l_acc[r] = jnp.where(lane == 0, total, 0.0)
            a_acc[r] = jnp.dot(weights, nv, preferred_element_type=F32)

    attend(
        False, owned, kv, group, slot_ref, len_ref, lambda e: q_ref[e], first,
        k_hbm, v_hbm, kbuf, vbuf, ksem, vsem, order, sbuf, hbuf, m_acc, l_acc, a_acc,
    )
    table = jnp.zeros((rows, 128), F32)
    for r in range(owned):
        total = jnp.sum(l_acc[r], axis=1, keepdims=True)
        out_ref[r] = (a_acc[r] / total).astype(BF16)
        table = jnp.where(lane % 32 == r, m_acc[r] * coef + jnp.log(total) * LOG2E, table)
    lse_ref[...] = table


def lent_kernel(
    owned, kv, group, slot_ref, len_ref, got_ref, own_ref, lse_ref, k_hbm, v_hbm,
    out_ref, info_ref, kbuf, vbuf, ksem, vsem, order, sbuf, hbuf, m_acc, l_acc, a_acc,
):
    rows, head = out_ref.shape[1:]
    coef = head ** -0.5 * LOG2E
    me = lax.axis_index("ctx")

    shift = MAXB.bit_length() - 1

    def find(s, rid):
        code = slot_ref[s]
        r = lax.shift_right_arithmetic(code, shift)
        inside = (r >= me * owned) & (r < (me + 1) * owned)
        return jnp.where((code >= 0) & jnp.logical_not(inside), r, rid)

    rid = lax.fori_loop(0, slot_ref.shape[0], find, jnp.int32(0), unroll=8)
    owner = lax.div(rid, owned)
    most = got_ref[0, pl.ds(rows, 16), :].astype(F32)
    for c in range(1, got_ref.shape[0]):
        most = jnp.maximum(most, got_ref[c, pl.ds(rows, 16), :].astype(F32))
    info_ref[0] = jnp.max(most[:1]).astype(jnp.int32)
    sent = jnp.max(got_ref[owner, pl.ds(rows, 16), :].astype(F32)[1:2]).astype(jnp.int32)
    info_ref[1] = (sent == lax.rem(rid, owned)).astype(jnp.int32)

    def first():
        m_acc[0] = jnp.full((rows, 128), NEG, F32)
        l_acc[0] = jnp.zeros((rows, 128), F32)
        a_acc[0] = jnp.zeros((rows, head), F32)
        out_ref[pl.ds(0, owned)] = own_ref[...]

    attend(
        True, owned, kv, group, slot_ref, len_ref, lambda e: got_ref[owner, pl.ds(0, rows), :], first,
        k_hbm, v_hbm, kbuf, vbuf, ksem, vsem, order, sbuf, hbuf, m_acc, l_acc, a_acc,
    )
    total = jnp.sum(l_acc[0], axis=1, keepdims=True)
    some = total > 0.0
    total = jnp.where(some, total, 1.0)
    out_ref[owned] = (a_acc[0] / total).astype(BF16)
    lse = jnp.where(some, m_acc[0] * coef + jnp.log(total) * LOG2E, NEG)
    lane = lax.broadcasted_iota(jnp.int32, (rows, 128), 1)
    table = jnp.where(lane % 32 == owned, lse, lse_ref[...])
    table = jnp.where(lane % 32 == owned + 1, rid.astype(F32), table)
    second = table - table.astype(BF16).astype(F32)
    third = second - second.astype(BF16).astype(F32)
    out_ref[owned + 1] = jnp.where(lane < 32, table, jnp.where(lane < 64, second, third)).astype(BF16)


def project_kernel(
    owned, steps, heads, sources, parts, *refs
):
    pieces = refs[:sources]
    w_hbm, send_ref, keep_ref, full, lse, flat, wbuf, wsem = refs[sources:]
    me = lax.axis_index("ctx")
    mine = lax.axis_index("tp")
    rows = steps * heads
    head = full.shape[1]
    span = owned * rows
    per = sources // parts
    copy = pltpu.make_async_copy(w_hbm, wbuf, wsem)
    copy.start()

    def spot(c):
        return (lax.div(c, per) ^ mine) * per + lax.rem(c, per)

    lane = lax.broadcasted_iota(jnp.int32, (rows, 128), 1)
    for d in range(sources):
        start = pl.multiple_of(spot(me ^ d) * span, span)
        full[pl.ds(start, span), :] = pieces[d][pl.ds(0, owned)].astype(F32).reshape(span, head)
    rids = []
    theirs = []
    for d in range(sources):
        packed = pieces[d][owned + 1].astype(F32)
        table = packed + pltpu.roll(packed, 96, 1) + pltpu.roll(packed, 64, 1)
        lse[me ^ d] = table
        theirs.append(jnp.sum(jnp.where(lane == owned, table, 0.0), axis=1, keepdims=True))
        rids.append(jnp.max(jnp.where(lane[:8] == owned + 1, table[:8], -1.0)).astype(jnp.int32))
    for d in range(sources):
        c = lax.div(rids[d], owned)
        r = lax.rem(rids[d], owned)
        start = pl.multiple_of((spot(c) * owned + r) * rows, rows)
        table = lse[c]
        left = jnp.sum(jnp.where(lane == r, table, 0.0), axis=1, keepdims=True)
        right = theirs[d]
        peak = jnp.maximum(left, right)
        w_left = jnp.exp2(left - peak)
        w_right = jnp.exp2(right - peak)
        total = w_left + w_right
        full[pl.ds(start, rows), :] = full[pl.ds(start, rows), :] * (w_left / total) + pieces[
            d
        ][owned].astype(F32) * (w_right / total)
        lse[c] = jnp.where(lane == r, peak + jnp.log(total) * LOG2E, table)
    count = sources * owned * steps
    for h in range(heads):
        flat[:, h * head : (h + 1) * head] = full[pl.ds(h, count, stride=heads), :].astype(BF16)
    copy.wait()
    result = jnp.dot(flat[...], wbuf[...], preferred_element_type=F32).astype(BF16)
    kept = count // parts
    for b in range(parts):
        target = keep_ref if b % 2 == 0 else send_ref
        target[b // 2] = result[b * kept : (b + 1) * kept]


def smem():
    return pl.BlockSpec(memory_space=pltpu.SMEM)


def vmem():
    return pl.BlockSpec(memory_space=pltpu.VMEM)


def hbm():
    return pl.BlockSpec(memory_space=pltpu.HBM)


def in_hbm(x):
    return pltpu.with_memory_space_constraint(x, pltpu.HBM)


def per_device(
    queries, new_keys, new_values, key_pool, value_pool, slot_block, lengths, out_weight
):
    owned, steps, heads, head = queries.shape
    kv = new_keys.shape[2]
    group = heads // kv
    slots, block_len = key_pool.shape[:2]
    sources = lax.axis_size("ctx")
    parts = lax.axis_size("tp")
    rows = steps * heads
    cols = out_weight.shape[1]
    q = queries.reshape(owned, rows, head)
    nk = in_hbm(new_keys.reshape(owned * steps * kv, head))
    nv = in_hbm(new_values.reshape(owned * steps * kv, head))
    keys = in_hbm(key_pool.reshape(slots, block_len * kv, head))
    values = in_hbm(value_pool.reshape(slots, block_len * kv, head))
    weight = in_hbm(out_weight)

    def ask(turn):
        message = pl.pallas_call(
            functools.partial(request_kernel, owned, rows, block_len),
            out_shape=jax.ShapeDtypeStruct((sources, rows + 16, head), BF16),
            in_specs=[smem(), smem(), smem(), vmem()],
            out_specs=vmem(),
            scratch_shapes=[pltpu.SMEM((owned + 1,), jnp.int32)],
            name="ask",
        )(turn, slot_block, lengths, q)
        return lax.all_to_all(message, "ctx", split_axis=0, concat_axis=0, tiled=True)

    cost = pl.CostEstimate(flops=COST, bytes_accessed=key_pool.size * 4, transcendentals=0)

    def buffers(sets):
        return [
            pltpu.VMEM((slots, block_len * kv, head), BF16),
            pltpu.VMEM((slots, block_len * kv, head), BF16),
            pltpu.SemaphoreType.DMA((slots,)),
            pltpu.SemaphoreType.DMA((slots,)),
            pltpu.SMEM((slots + 1,), jnp.int32),
            pltpu.VMEM((2, GROUP // 2, 2 * rows, block_len * kv), F32),
            pltpu.VMEM((2, GROUP // 2, 2 * rows, 128), F32),
            pltpu.VMEM((sets, rows, 128), F32),
            pltpu.VMEM((sets, rows, 128), F32),
            pltpu.VMEM((sets, rows, head), F32),
        ]

    got = ask(jnp.zeros((1,), jnp.int32))
    own, lse = pl.pallas_call(
        functools.partial(own_kernel, owned, steps, kv, group),
        out_shape=(
            jax.ShapeDtypeStruct((owned, rows, head), BF16),
            jax.ShapeDtypeStruct((rows, 128), F32),
        ),
        in_specs=[smem(), smem(), vmem(), hbm(), hbm(), hbm(), hbm()],
        out_specs=(vmem(), vmem()),
        scratch_shapes=[
            pltpu.VMEM(nk.shape, BF16),
            pltpu.VMEM(nv.shape, BF16),
            pltpu.SemaphoreType.DMA((2,)),
        ]
        + buffers(owned),
        cost_estimate=cost,
        name="own",
        compiler_params=pltpu.CompilerParams(vmem_limit_bytes=40 * 2**20),
    )(slot_block, lengths, q, nk, nv, keys, values)

    def answer(got):
        return pl.pallas_call(
            functools.partial(lent_kernel, owned, kv, group),
            out_shape=(
                jax.ShapeDtypeStruct((owned + 2, rows, head), BF16),
                jax.ShapeDtypeStruct((2,), jnp.int32),
            ),
            in_specs=[smem(), smem(), vmem(), vmem(), vmem(), hbm(), hbm()],
            out_specs=(vmem(), smem()),
            scratch_shapes=buffers(1),
            cost_estimate=cost,
            name="lent",
            compiler_params=pltpu.CompilerParams(vmem_limit_bytes=40 * 2**20),
        )(slot_block, lengths, got, own, lse, keys, values)

    partial, info = answer(got)

    def more(state):
        return state[0] < state[1]

    def next_round(state):
        turn, rounds, held = state
        fresh, info = answer(ask(turn.reshape(1)))
        return turn + 1, rounds, jnp.where(info[1] > 0, fresh, held)

    _, _, partial = lax.while_loop(more, next_round, (jnp.int32(1), info[0], partial))

    pieces = [partial]
    for d in range(1, sources):
        bit = d & -d
        pieces.append(lax.ppermute(pieces[d ^ bit], "ctx", [(i, i ^ bit) for i in range(sources)]))
    count = sources * owned * steps
    kept = count // parts
    send, keep = pl.pallas_call(
        functools.partial(project_kernel, owned, steps, heads, sources, parts),
        out_shape=(
            jax.ShapeDtypeStruct((parts // 2, kept, cols), BF16),
            jax.ShapeDtypeStruct((parts // 2, kept, cols), BF16),
        ),
        in_specs=[vmem()] * sources + [hbm()],
        out_specs=(vmem(), vmem()),
        scratch_shapes=[
            pltpu.VMEM((sources * owned * rows, head), F32),
            pltpu.VMEM((sources, rows, 128), F32),
            pltpu.VMEM((count, heads * head), BF16),
            pltpu.VMEM(out_weight.shape, BF16),
            pltpu.SemaphoreType.DMA,
        ],
        name="project",
        compiler_params=pltpu.CompilerParams(vmem_limit_bytes=48 * 2**20),
    )(*pieces, weight)

    bit = 1
    while True:
        other = lax.ppermute(send, "tp", [(i, i ^ bit) for i in range(parts)])
        held = keep.astype(F32) + other.astype(F32)
        bit *= 2
        if bit == parts:
            break
        held = held.reshape((held.shape[0] // 2, 2) + held.shape[1:])
        send, keep = held[:, 1].astype(BF16), held[:, 0]
    return held.astype(BF16).reshape(kept // steps, steps, cols)


def solution(mesh):
    return jax.shard_map(
        per_device,
        mesh=mesh,
        in_specs=(
            P("ctx", None, "tp", None),
            P("ctx", None, "tp", None),
            P("ctx", None, "tp", None),
            P("ctx", None, "tp", None),
            P("ctx", None, "tp", None),
            P("ctx"),
            P(),
            P("tp", "ctx"),
        ),
        out_specs=P("tp", None, "ctx"),
        check_vma=False,
    )
```

profile of v0, /device:TPU:0, one launch (start us, length us, event | category | flops | bytes accessed | tf_op | source)
XLA Modules:
  0.0 65.8 jit_solution(15444696138565478378)
XLA Ops:
  0.0 2.0 %ask.2 = bf16[8,80,128]{2,1,0:T(8,128)(2,1)} custom-call(s32[1]{0:T(128)} %constant.8.clone.1.round_ref, s32[64]{0:T(128)} %slot_ref.5, s32[64]{0:T(128)} %len_ref.5, bf16[8,64,128]{2,1,0:T(8,128)(2,1)} %bitcast.23), custom_call_target="tpu_custom_call" | custom-call | tf_op jit(solution)/shard_map/ask/pallas_call | solution.py:351
  2.0 7.3 %all-to-all-start.1 = ((bf16[8,80,128]{2,1,0:T(8,128)(2,1)}), bf16[8,80,128]{2,1,0:T(8,128)(2,1)S(1)}, u32[]{:S(2)}, u32[]{:S(2)}) async-start(bf16[8,80,128]{2,1,0:T(8,128)(2,1)} %ask.2), calls=%async_computation.1 | async-start | bytes 327680 | tf_op jit(solution)/shard_map/all_to_all | solution.py:359
  9.3 7.4 %own.1 = (bf16[8,64,128]{2,1,0:T(8,128)(2,1)S(1)}, f32[64,128]{1,0:T(8,128)S(1)}) custom-call(s32[64]{0:T(128)} %slot_ref.5, s32[64]{0:T(128)} %len_ref.5, bf16[8,64,128]{2,1,0:T(8,128)(2,1)} %bitcast.24, bf16[64,128]{1,0:T(8,128)(2,1)} %bitcast.32, bf16[64,128]{1,0:T(8,128)(2,1)} %bitcast.33, bf16[64,512,128]{2,1,0:T(8,128)(2,1)} %bitcast.26, ...), custom_call_target="tpu_custom_call" | custom-call | flops 10000000000 | bytes 16777216 | tf_op jit(solution)/shard_map/own/pallas_call | solution.py:378
  16.6 0.2 all-to-all-done.1.got_ref
  16.8 2.8 %lent.2 = (bf16[10,64,128]{2,1,0:T(8,128)(2,1)S(1)}, s32[2]{0:T(128)}) custom-call(s32[64]{0:T(128)S(1)} %copy-done.1, s32[64]{0:T(128)S(1)} %copy-done.2, bf16[8,80,128]{2,1,0:T(8,128)(2,1)S(1)} %all-to-all-done.1.got_ref, bf16[8,64,128]{2,1,0:T(8,128)(2,1)S(1)} %get-tuple-element.165.own_ref, f32[64,128]{1,0:T(8,128)S(1)} %get-tuple-element.166.lse_ref, ...), custom_call_target="tpu_custom_call" | custom-call | flops 10000000000 | bytes 16777216 | tf_op jit(solution)/shard_map/lent/pallas_call | solution.py:398
  19.7 0.6 while.10
  20.3 7.8 %collective-permute-start.3 = (bf16[10,64,128]{2,1,0:T(8,128)(2,1)S(1)}, bf16[10,64,128]{2,1,0:T(8,128)(2,1)S(1)}, u32[]{:S(2)}, u32[]{:S(2)}) collective-permute-start(bf16[10,64,128]{2,1,0:T(8,128)(2,1)S(1)} %get-tuple-element.70.refs_0_), channel_id=1, source_target_pairs={{0,16},{4,20},{8,24},{12,28},{16,0},{20,4},{24,8},{28,12},{1,17},{... | collective-permute-start | bytes 491528 | tf_op jit(solution)/shard_map/ppermute | solution.py:427
  28.1 5.4 %collective-permute-start.1 = (bf16[10,64,128]{2,1,0:T(8,128)(2,1)S(1)}, bf16[10,64,128]{2,1,0:T(8,128)(2,1)S(1)}, u32[]{:S(2)}, u32[]{:S(2)}) collective-permute-start(bf16[10,64,128]{2,1,0:T(8,128)(2,1)S(1)} %get-tuple-element.70.refs_0_), channel_id=1, source_target_pairs={{0,8},{4,12},{8,0},{12,4},{16,24},{20,28},{24,16},{28,20},{1,9},{5... | collective-permute-start | bytes 491528 | tf_op jit(solution)/shard_map/ppermute | solution.py:427
  33.5 5.0 %collective-permute-start.5 = (bf16[10,64,128]{2,1,0:T(8,128)(2,1)S(1)}, bf16[10,64,128]{2,1,0:T(8,128)(2,1)S(1)}, u32[]{:S(2)}, u32[]{:S(2)}) collective-permute-start(bf16[10,64,128]{2,1,0:T(8,128)(2,1)S(1)} %collective-permute-done.3.refs_4_), channel_id=1, source_target_pairs={{0,8},{4,12},{8,0},{12,4},{16,24},{20,28},{24,16},{28,20},{1,9},{5... | collective-permute-start | bytes 491528 | tf_op jit(solution)/shard_map/ppermute | solution.py:427
  38.5 0.5 collective-permute-start
  39.0 1.5 %collective-permute-start.4 = (bf16[10,64,128]{2,1,0:T(8,128)(2,1)S(1)}, bf16[10,64,128]{2,1,0:T(8,128)(2,1)S(1)}, u32[]{:S(2)}, u32[]{:S(2)}) collective-permute-start(bf16[10,64,128]{2,1,0:T(8,128)(2,1)S(1)} %collective-permute-done.3.refs_4_), channel_id=1, source_target_pairs={{0,4},{4,0},{8,12},{12,8},{16,20},{20,16},{24,28},{28,24},{1,5},{5... | collective-permute-start | bytes 491528 | tf_op jit(solution)/shard_map/ppermute | solution.py:427
  40.6 0.5 collective-permute-start.2
  41.1 0.8 %collective-permute-done.5.refs_6_ = bf16[10,64,128]{2,1,0:T(8,128)(2,1)S(1)} collective-permute-done((bf16[10,64,128]{2,1,0:T(8,128)(2,1)S(1)}, bf16[10,64,128]{2,1,0:T(8,128)(2,1)S(1)}, u32[]{:S(2)}, u32[]{:S(2)}) %collective-permute-start.5) | collective-permute-done | bytes 163872 | tf_op jit(solution)/shard_map/ppermute | solution.py:427
  41.8 1.0 %collective-permute-start.6 = (bf16[10,64,128]{2,1,0:T(8,128)(2,1)S(1)}, bf16[10,64,128]{2,1,0:T(8,128)(2,1)S(1)}, u32[]{:S(2)}, u32[]{:S(2)}) collective-permute-start(bf16[10,64,128]{2,1,0:T(8,128)(2,1)S(1)} %collective-permute-done.5.refs_6_), channel_id=1, source_target_pairs={{0,4},{4,0},{8,12},{12,8},{16,20},{20,16},{24,28},{28,24},{1,5},{5... | collective-permute-start | bytes 491528 | tf_op jit(solution)/shard_map/ppermute | solution.py:427
  42.8 2.8 %collective-permute-done.refs_1_ = bf16[10,64,128]{2,1,0:T(8,128)(2,1)S(1)} collective-permute-done((bf16[10,64,128]{2,1,0:T(8,128)(2,1)S(1)}, bf16[10,64,128]{2,1,0:T(8,128)(2,1)S(1)}, u32[]{:S(2)}, u32[]{:S(2)}) %collective-permute-start) | collective-permute-done | bytes 163872 | tf_op jit(solution)/shard_map/ppermute | solution.py:427
  45.6 3.5 %collective-permute-done.4.refs_5_ = bf16[10,64,128]{2,1,0:T(8,128)(2,1)S(1)} collective-permute-done((bf16[10,64,128]{2,1,0:T(8,128)(2,1)S(1)}, bf16[10,64,128]{2,1,0:T(8,128)(2,1)S(1)}, u32[]{:S(2)}, u32[]{:S(2)}) %collective-permute-start.4) | collective-permute-done | bytes 163872 | tf_op jit(solution)/shard_map/ppermute | solution.py:427
  49.1 2.2 %collective-permute-done.2.refs_3_ = bf16[10,64,128]{2,1,0:T(8,128)(2,1)S(1)} collective-permute-done((bf16[10,64,128]{2,1,0:T(8,128)(2,1)S(1)}, bf16[10,64,128]{2,1,0:T(8,128)(2,1)S(1)}, u32[]{:S(2)}, u32[]{:S(2)}) %collective-permute-start.2) | collective-permute-done | bytes 163872 | tf_op jit(solution)/shard_map/ppermute | solution.py:427
  51.3 1.8 %collective-permute-done.6.refs_7_ = bf16[10,64,128]{2,1,0:T(8,128)(2,1)S(1)} collective-permute-done((bf16[10,64,128]{2,1,0:T(8,128)(2,1)S(1)}, bf16[10,64,128]{2,1,0:T(8,128)(2,1)S(1)}, u32[]{:S(2)}, u32[]{:S(2)}) %collective-permute-start.6) | collective-permute-done | bytes 163872 | tf_op jit(solution)/shard_map/ppermute | solution.py:427
  53.1 4.7 %project.1 = (bf16[2,64,1024]{2,1,0:T(8,128)(2,1)S(1)}, bf16[2,64,1024]{2,1,0:T(8,128)(2,1)S(1)}) custom-call(bf16[10,64,128]{2,1,0:T(8,128)(2,1)S(1)} %get-tuple-element.70.refs_0_, bf16[10,64,128]{2,1,0:T(8,128)(2,1)S(1)} %collective-permute-done.refs_1_, bf16[10,64,128]{2,1,0:T(8,128)(2,1)S(1)} %collective-permute-done.1.refs_2_, ...), custom_call_target="tpu_custom_call" | custom-call | tf_op jit(solution)/shard_map/project/pallas_call | solution.py:430
  57.8 0.1 collective-permute-start.7
  57.8 1.5 %collective-permute-done.7 = bf16[2,64,1024]{2,1,0:T(8,128)(2,1)S(1)} collective-permute-done((bf16[2,64,1024]{2,1,0:T(8,128)(2,1)S(1)}, bf16[2,64,1024]{2,1,0:T(8,128)(2,1)S(1)}, u32[]{:S(2)}, u32[]{:S(2)}) %collective-permute-start.7) | collective-permute-done | bytes 262176 | tf_op jit(solution)/shard_map/ppermute | solution.py:451
  59.5 1.6 %collective-permute-start.8 = (bf16[1,64,1024]{2,1,0:T(8,128)(2,1)S(1)}, bf16[1,64,1024]{2,1,0:T(8,128)(2,1)S(1)}, u32[]{:S(2)}, u32[]{:S(2)}) collective-permute-start(bf16[1,64,1024]{2,1,0:T(8,128)(2,1)S(1)} %fusion.2), channel_id=1, source_target_pairs={{0,2},{1,3},{2,0},{3,1},{4,6},{5,7},{6,4},{7,5},{8,10},{9,11},{10,... | collective-permute-start | bytes 393224 | tf_op jit(solution)/shard_map/ppermute | solution.py:451
  61.1 4.0 %collective-permute-done.8 = bf16[1,64,1024]{2,1,0:T(8,128)(2,1)S(1)} collective-permute-done((bf16[1,64,1024]{2,1,0:T(8,128)(2,1)S(1)}, bf16[1,64,1024]{2,1,0:T(8,128)(2,1)S(1)}, u32[]{:S(2)}, u32[]{:S(2)}) %collective-permute-start.8) | collective-permute-done | bytes 131104 | tf_op jit(solution)/shard_map/ppermute | solution.py:451
  65.1 0.7 %reshape.45 = bf16[16,4,1024]{2,1,0:T(4,128)(2,1)} reshape(bf16[1,64,1024]{2,1,0:T(8,128)(2,1)S(1)} %fusion.1) | data formatting | bytes 262144 | tf_op jit(solution)/shard_map/reshape | solution.py:458
  (11 shorter events, 0.1 us)
Async XLA Ops:
  2.0 14.8 %all-to-all-start.1 = ((bf16[8,80,128]{2,1,0:T(8,128)(2,1)}), bf16[8,80,128]{2,1,0:T(8,128)(2,1)S(1)}, u32[]{:S(2)}, u32[]{:S(2)}) async-start(bf16[8,80,128]{2,1,0:T(8,128)(2,1)} %ask.2), calls=%async_computation.1 | async-start | bytes 327680 | tf_op jit(solution)/shard_map/all_to_all | solution.py:359
  9.2 7.6 %copy-start.1 = (s32[64]{0:T(128)S(1)}, s32[64]{0:T(128)}, u32[]{:S(2)}) copy-start(s32[64]{0:T(128)} %slot_ref.5) | copy-start | bytes 772
  9.3 7.6 %copy-start.2 = (s32[64]{0:T(128)S(1)}, s32[64]{0:T(128)}, u32[]{:S(2)}) copy-start(s32[64]{0:T(128)} %len_ref.5) | copy-start | bytes 772
  16.8 2.8 %copy-start = (bf16[8,4,16,128]{3,2,1,0:T(8,128)(2,1)S(1)}, bf16[8,4,16,128]{3,2,1,0:T(8,128)(2,1)}, u32[]{:S(2)}) copy-start(bf16[8,4,16,128]{3,2,1,0:T(8,128)(2,1)} %param.10) | copy-start | bytes 393220
  20.3 13.2 %collective-permute-start.3 = (bf16[10,64,128]{2,1,0:T(8,128)(2,1)S(1)}, bf16[10,64,128]{2,1,0:T(8,128)(2,1)S(1)}, u32[]{:S(2)}, u32[]{:S(2)}) collective-permute-start(bf16[10,64,128]{2,1,0:T(8,128)(2,1)S(1)} %get-tuple-element.70.refs_0_), channel_id=1, source_target_pairs={{0,16},{4,20},{8,24},{12,28},{16,0},{20,4},{24,8},{28,12},{1,17},{... | collective-permute-start | bytes 491528 | tf_op jit(solution)/shard_map/ppermute | solution.py:427
  28.1 12.4 %collective-permute-start.1 = (bf16[10,64,128]{2,1,0:T(8,128)(2,1)S(1)}, bf16[10,64,128]{2,1,0:T(8,128)(2,1)S(1)}, u32[]{:S(2)}, u32[]{:S(2)}) collective-permute-start(bf16[10,64,128]{2,1,0:T(8,128)(2,1)S(1)} %get-tuple-element.70.refs_0_), channel_id=1, source_target_pairs={{0,8},{4,12},{8,0},{12,4},{16,24},{20,28},{24,16},{28,20},{1,9},{5... | collective-permute-start | bytes 491528 | tf_op jit(solution)/shard_map/ppermute | solution.py:427
  33.5 8.3 %collective-permute-start.5 = (bf16[10,64,128]{2,1,0:T(8,128)(2,1)S(1)}, bf16[10,64,128]{2,1,0:T(8,128)(2,1)S(1)}, u32[]{:S(2)}, u32[]{:S(2)}) collective-permute-start(bf16[10,64,128]{2,1,0:T(8,128)(2,1)S(1)} %collective-permute-done.3.refs_4_), channel_id=1, source_target_pairs={{0,8},{4,12},{8,0},{12,4},{16,24},{20,28},{24,16},{28,20},{1,9},{5... | collective-permute-start | bytes 491528 | tf_op jit(solution)/shard_map/ppermute | solution.py:427
  38.5 7.1 %collective-permute-start = (bf16[10,64,128]{2,1,0:T(8,128)(2,1)S(1)}, bf16[10,64,128]{2,1,0:T(8,128)(2,1)S(1)}, u32[]{:S(2)}, u32[]{:S(2)}) collective-permute-start(bf16[10,64,128]{2,1,0:T(8,128)(2,1)S(1)} %get-tuple-element.70.refs_0_), channel_id=1, source_target_pairs={{0,4},{4,0},{8,12},{12,8},{16,20},{20,16},{24,28},{28,24},{1,5},{5... | collective-permute-start | bytes 491528 | tf_op jit(solution)/shard_map/ppermute | solution.py:427
  39.0 10.1 %collective-permute-start.4 = (bf16[10,64,128]{2,1,0:T(8,128)(2,1)S(1)}, bf16[10,64,128]{2,1,0:T(8,128)(2,1)S(1)}, u32[]{:S(2)}, u32[]{:S(2)}) collective-permute-start(bf16[10,64,128]{2,1,0:T(8,128)(2,1)S(1)} %collective-permute-done.3.refs_4_), channel_id=1, source_target_pairs={{0,4},{4,0},{8,12},{12,8},{16,20},{20,16},{24,28},{28,24},{1,5},{5... | collective-permute-start | bytes 491528 | tf_op jit(solution)/shard_map/ppermute | solution.py:427
  40.6 10.8 %collective-permute-start.2 = (bf16[10,64,128]{2,1,0:T(8,128)(2,1)S(1)}, bf16[10,64,128]{2,1,0:T(8,128)(2,1)S(1)}, u32[]{:S(2)}, u32[]{:S(2)}) collective-permute-start(bf16[10,64,128]{2,1,0:T(8,128)(2,1)S(1)} %collective-permute-done.1.refs_2_), channel_id=1, source_target_pairs={{0,4},{4,0},{8,12},{12,8},{16,20},{20,16},{24,28},{28,24},{1,5},{5... | collective-permute-start | bytes 491528 | tf_op jit(solution)/shard_map/ppermute | solution.py:427
  41.8 11.3 %collective-permute-start.6 = (bf16[10,64,128]{2,1,0:T(8,128)(2,1)S(1)}, bf16[10,64,128]{2,1,0:T(8,128)(2,1)S(1)}, u32[]{:S(2)}, u32[]{:S(2)}) collective-permute-start(bf16[10,64,128]{2,1,0:T(8,128)(2,1)S(1)} %collective-permute-done.5.refs_6_), channel_id=1, source_target_pairs={{0,4},{4,0},{8,12},{12,8},{16,20},{20,16},{24,28},{28,24},{1,5},{5... | collective-permute-start | bytes 491528 | tf_op jit(solution)/shard_map/ppermute | solution.py:427
  57.8 1.6 %collective-permute-start.7 = (bf16[2,64,1024]{2,1,0:T(8,128)(2,1)S(1)}, bf16[2,64,1024]{2,1,0:T(8,128)(2,1)S(1)}, u32[]{:S(2)}, u32[]{:S(2)}) collective-permute-start(bf16[2,64,1024]{2,1,0:T(8,128)(2,1)S(1)} %get-tuple-element.72), channel_id=1, source_target_pairs={{0,1},{1,0},{2,3},{3,2},{4,5},{5,4},{6,7},{7,6},{8,9},{9,8},{10,11... | collective-permute-start | bytes 786440 | tf_op jit(solution)/shard_map/ppermute | solution.py:451
  59.5 5.6 %collective-permute-start.8 = (bf16[1,64,1024]{2,1,0:T(8,128)(2,1)S(1)}, bf16[1,64,1024]{2,1,0:T(8,128)(2,1)S(1)}, u32[]{:S(2)}, u32[]{:S(2)}) collective-permute-start(bf16[1,64,1024]{2,1,0:T(8,128)(2,1)S(1)} %fusion.2), channel_id=1, source_target_pairs={{0,2},{1,3},{2,0},{3,1},{4,6},{5,7},{6,4},{7,5},{8,10},{9,11},{10,... | collective-permute-start | bytes 393224 | tf_op jit(solution)/shard_map/ppermute | solution.py:451
where the time goes:
time: 66.1 us; the launch traced here: 65.8 us
  starting transfers between devices  30.7 us (46%)
  Pallas kernels  16.8 us (25%)
  waiting for transfers between devices  16.7 us (25%)
  local copies, waits for them, and re-layouts  0.74 us (1%)
    ppermute x7, starting transfers between devices, per_device(): lax.ppermute(pieces[d ^ bit], 'ctx', [(i, i ^ bit) for i in range(sources)])  21.8 us
    ppermute x7, waiting for transfers between devices, per_device(): lax.ppermute(pieces[d ^ bit], 'ctx', [(i, i ^ bit) for i in range(sources)])  11 us
    pallas_call x1, Pallas kernels, per_device(): pl.pallas_call(functools.partial(own_kernel, owned, steps, kv, group), ou...  7.36 us
    all_to_all x1, starting transfers between devices, ask(): lax.all_to_all(message, 'ctx', split_axis=0, concat_axis=0, tiled=True)  7.28 us
    ppermute x2, waiting for transfers between devices, per_device(): other = lax.ppermute(send, 'tp', [(i, i ^ bit) for i in range(parts)])  5.52 us
    pallas_call x1, Pallas kernels, per_device(): pl.pallas_call(functools.partial(project_kernel, owned, steps, heads, sou...  4.67 us
    pallas_call x1, Pallas kernels, answer(): pl.pallas_call(functools.partial(lent_kernel, owned, kv, group), out_shap...  2.83 us
    pallas_call x1, Pallas kernels, ask(): pl.pallas_call(functools.partial(request_kernel, owned, rows, block_len),...  1.97 us
  transfers between devices with their start and end apart: 10, of which 8 were waited for; matrix products, arithmetic and copies ran while one was open for 0% of the time, Pallas kernels for 11%

commit v1 on v0

--- a/solution.py
+++ b/solution.py
@@ -226,8 +226,8 @@
         inside = (r >= me * owned) & (r < (me + 1) * owned)
         return jnp.where((code >= 0) & jnp.logical_not(inside), r, rid)
 
-    rid = lax.fori_loop(0, slot_ref.shape[0], find, jnp.int32(0), unroll=8)
-    owner = lax.div(rid, owned)
+    rid = lax.fori_loop(0, slot_ref.shape[0], find, jnp.int32(-1), unroll=8)
+    owner = lax.div(jnp.maximum(rid, 0), owned)
     most = got_ref[0, pl.ds(rows, 16), :].astype(F32)
     for c in range(1, got_ref.shape[0]):
         most = jnp.maximum(most, got_ref[c, pl.ds(rows, 16), :].astype(F32))
@@ -288,20 +288,23 @@
         theirs.append(jnp.sum(jnp.where(lane == owned, table, 0.0), axis=1, keepdims=True))
         rids.append(jnp.max(jnp.where(lane[:8] == owned + 1, table[:8], -1.0)).astype(jnp.int32))
     for d in range(sources):
-        c = lax.div(rids[d], owned)
-        r = lax.rem(rids[d], owned)
-        start = pl.multiple_of((spot(c) * owned + r) * rows, rows)
-        table = lse[c]
-        left = jnp.sum(jnp.where(lane == r, table, 0.0), axis=1, keepdims=True)
-        right = theirs[d]
-        peak = jnp.maximum(left, right)
-        w_left = jnp.exp2(left - peak)
-        w_right = jnp.exp2(right - peak)
-        total = w_left + w_right
-        full[pl.ds(start, rows), :] = full[pl.ds(start, rows), :] * (w_left / total) + pieces[
-            d
-        ][owned].astype(F32) * (w_right / total)
-        lse[c] = jnp.where(lane == r, peak + jnp.log(total) * LOG2E, table)
+
+        @pl.when(rids[d] >= 0)
+        def _(d=d):
+            c = lax.div(rids[d], owned)
+            r = lax.rem(rids[d], owned)
+            start = pl.multiple_of((spot(c) * owned + r) * rows, rows)
+            table = lse[c]
+            left = jnp.sum(jnp.where(lane == r, table, 0.0), axis=1, keepdims=True)
+            right = theirs[d]
+            peak = jnp.maximum(left, right)
+            w_left = jnp.exp2(left - peak)
+            w_right = jnp.exp2(right - peak)
+            total = w_left + w_right
+            full[pl.ds(start, rows), :] = full[pl.ds(start, rows), :] * (w_left / total) + pieces[
+                d
+            ][owned].astype(F32) * (w_right / total)
+            lse[c] = jnp.where(lane == r, peak + jnp.log(total) * LOG2E, table)
     count = sources * owned * steps
     for h in range(heads):
         flat[:, h * head : (h + 1) * head] = full[pl.ds(h, count, stride=heads), :].astype(BF16)

time: 66.1 us -> 65.4 us (0.989)
  Pallas kernels: 16.8 us -> 16.1 us
    pallas_call x1, Pallas kernels: 4.67 us -> 3.95 us  [per_device(): pl.pallas_call(functools.partial(project_kernel, owned, steps, heads, sou...]
where the time goes in v1:
time: 65.4 us; the launch traced here: 65.1 us
  starting transfers between devices  30.7 us (47%)
  waiting for transfers between devices  16.7 us (26%)
  Pallas kernels  16.1 us (25%)
  local copies, waits for them, and re-layouts  0.74 us (1%)
    ppermute x7, starting transfers between devices, per_device(): lax.ppermute(pieces[d ^ bit], 'ctx', [(i, i ^ bit) for i in range(sources)])  21.8 us
    ppermute x7, waiting for transfers between devices, per_device(): lax.ppermute(pieces[d ^ bit], 'ctx', [(i, i ^ bit) for i in range(sources)])  11 us
    pallas_call x1, Pallas kernels, per_device(): pl.pallas_call(functools.partial(own_kernel, owned, steps, kv, group), ou...  7.36 us
    all_to_all x1, starting transfers between devices, ask(): lax.all_to_all(message, 'ctx', split_axis=0, concat_axis=0, tiled=True)  7.28 us
    ppermute x2, waiting for transfers between devices, per_device(): other = lax.ppermute(send, 'tp', [(i, i ^ bit) for i in range(parts)])  5.52 us
    pallas_call x1, Pallas kernels, per_device(): pl.pallas_call(functools.partial(project_kernel, owned, steps, heads, sou...  3.95 us
    pallas_call x1, Pallas kernels, answer(): pl.pallas_call(functools.partial(lent_kernel, owned, kv, group), out_shap...  2.83 us
    pallas_call x1, Pallas kernels, ask(): pl.pallas_call(functools.partial(request_kernel, owned, rows, block_len),...  1.97 us
  transfers between devices with their start and end apart: 10, of which 8 were waited for; matrix products, arithmetic and copies ran while one was open for 0% of the time, Pallas kernels for 11%

profile of v1, /device:TPU:0, one launch (start us, length us, event | category | flops | bytes accessed | tf_op | source)
XLA Modules:
  0.0 65.1 jit_solution(8030149086059516918)
XLA Ops:
  0.0 2.0 %ask.2 = bf16[8,80,128]{2,1,0:T(8,128)(2,1)} custom-call(s32[1]{0:T(128)} %constant.8.clone.1.round_ref, s32[64]{0:T(128)} %slot_ref.5, s32[64]{0:T(128)} %len_ref.5, bf16[8,64,128]{2,1,0:T(8,128)(2,1)} %bitcast.23), custom_call_target="tpu_custom_call" | custom-call | tf_op jit(solution)/shard_map/ask/pallas_call | solution.py:354
  2.0 7.3 %all-to-all-start.1 = ((bf16[8,80,128]{2,1,0:T(8,128)(2,1)}), bf16[8,80,128]{2,1,0:T(8,128)(2,1)S(1)}, u32[]{:S(2)}, u32[]{:S(2)}) async-start(bf16[8,80,128]{2,1,0:T(8,128)(2,1)} %ask.2), calls=%async_computation.1 | async-start | bytes 327680 | tf_op jit(solution)/shard_map/all_to_all | solution.py:362
  9.3 7.4 %own.1 = (bf16[8,64,128]{2,1,0:T(8,128)(2,1)S(1)}, f32[64,128]{1,0:T(8,128)S(1)}) custom-call(s32[64]{0:T(128)} %slot_ref.5, s32[64]{0:T(128)} %len_ref.5, bf16[8,64,128]{2,1,0:T(8,128)(2,1)} %bitcast.24, bf16[64,128]{1,0:T(8,128)(2,1)} %bitcast.32, bf16[64,128]{1,0:T(8,128)(2,1)} %bitcast.33, bf16[64,512,128]{2,1,0:T(8,128)(2,1)} %bitcast.26, ...), custom_call_target="tpu_custom_call" | custom-call | flops 10000000000 | bytes 16777216 | tf_op jit(solution)/shard_map/own/pallas_call | solution.py:381
  16.6 0.2 all-to-all-done.1.got_ref
  16.8 2.8 %lent.2 = (bf16[10,64,128]{2,1,0:T(8,128)(2,1)S(1)}, s32[2]{0:T(128)}) custom-call(s32[64]{0:T(128)S(1)} %copy-done.1, s32[64]{0:T(128)S(1)} %copy-done.2, bf16[8,80,128]{2,1,0:T(8,128)(2,1)S(1)} %all-to-all-done.1.got_ref, bf16[8,64,128]{2,1,0:T(8,128)(2,1)S(1)} %get-tuple-element.165.own_ref, f32[64,128]{1,0:T(8,128)S(1)} %get-tuple-element.166.lse_ref, ...), custom_call_target="tpu_custom_call" | custom-call | flops 10000000000 | bytes 16777216 | tf_op jit(solution)/shard_map/lent/pallas_call | solution.py:401
  19.7 0.6 while.10
  20.3 7.8 %collective-permute-start.3 = (bf16[10,64,128]{2,1,0:T(8,128)(2,1)S(1)}, bf16[10,64,128]{2,1,0:T(8,128)(2,1)S(1)}, u32[]{:S(2)}, u32[]{:S(2)}) collective-permute-start(bf16[10,64,128]{2,1,0:T(8,128)(2,1)S(1)} %get-tuple-element.70.refs_0_), channel_id=1, source_target_pairs={{0,16},{4,20},{8,24},{12,28},{16,0},{20,4},{24,8},{28,12},{1,17},{... | collective-permute-start | bytes 491528 | tf_op jit(solution)/shard_map/ppermute | solution.py:430
  28.1 5.4 %collective-permute-start.1 = (bf16[10,64,128]{2,1,0:T(8,128)(2,1)S(1)}, bf16[10,64,128]{2,1,0:T(8,128)(2,1)S(1)}, u32[]{:S(2)}, u32[]{:S(2)}) collective-permute-start(bf16[10,64,128]{2,1,0:T(8,128)(2,1)S(1)} %get-tuple-element.70.refs_0_), channel_id=1, source_target_pairs={{0,8},{4,12},{8,0},{12,4},{16,24},{20,28},{24,16},{28,20},{1,9},{5... | collective-permute-start | bytes 491528 | tf_op jit(solution)/shard_map/ppermute | solution.py:430
  33.5 5.0 %collective-permute-start.5 = (bf16[10,64,128]{2,1,0:T(8,128)(2,1)S(1)}, bf16[10,64,128]{2,1,0:T(8,128)(2,1)S(1)}, u32[]{:S(2)}, u32[]{:S(2)}) collective-permute-start(bf16[10,64,128]{2,1,0:T(8,128)(2,1)S(1)} %collective-permute-done.3.refs_4_), channel_id=1, source_target_pairs={{0,8},{4,12},{8,0},{12,4},{16,24},{20,28},{24,16},{28,20},{1,9},{5... | collective-permute-start | bytes 491528 | tf_op jit(solution)/shard_map/ppermute | solution.py:430
  38.5 0.5 collective-permute-start
  39.0 1.5 %collective-permute-start.4 = (bf16[10,64,128]{2,1,0:T(8,128)(2,1)S(1)}, bf16[10,64,128]{2,1,0:T(8,128)(2,1)S(1)}, u32[]{:S(2)}, u32[]{:S(2)}) collective-permute-start(bf16[10,64,128]{2,1,0:T(8,128)(2,1)S(1)} %collective-permute-done.3.refs_4_), channel_id=1, source_target_pairs={{0,4},{4,0},{8,12},{12,8},{16,20},{20,16},{24,28},{28,24},{1,5},{5... | collective-permute-start | bytes 491528 | tf_op jit(solution)/shard_map/ppermute | solution.py:430
  40.6 0.5 collective-permute-start.2
  41.1 0.8 %collective-permute-done.5.refs_6_ = bf16[10,64,128]{2,1,0:T(8,128)(2,1)S(1)} collective-permute-done((bf16[10,64,128]{2,1,0:T(8,128)(2,1)S(1)}, bf16[10,64,128]{2,1,0:T(8,128)(2,1)S(1)}, u32[]{:S(2)}, u32[]{:S(2)}) %collective-permute-start.5) | collective-permute-done | bytes 163872 | tf_op jit(solution)/shard_map/ppermute | solution.py:430
  41.8 1.0 %collective-permute-start.6 = (bf16[10,64,128]{2,1,0:T(8,128)(2,1)S(1)}, bf16[10,64,128]{2,1,0:T(8,128)(2,1)S(1)}, u32[]{:S(2)}, u32[]{:S(2)}) collective-permute-start(bf16[10,64,128]{2,1,0:T(8,128)(2,1)S(1)} %collective-permute-done.5.refs_6_), channel_id=1, source_target_pairs={{0,4},{4,0},{8,12},{12,8},{16,20},{20,16},{24,28},{28,24},{1,5},{5... | collective-permute-start | bytes 491528 | tf_op jit(solution)/shard_map/ppermute | solution.py:430
  42.8 2.8 %collective-permute-done.refs_1_ = bf16[10,64,128]{2,1,0:T(8,128)(2,1)S(1)} collective-permute-done((bf16[10,64,128]{2,1,0:T(8,128)(2,1)S(1)}, bf16[10,64,128]{2,1,0:T(8,128)(2,1)S(1)}, u32[]{:S(2)}, u32[]{:S(2)}) %collective-permute-start) | collective-permute-done | bytes 163872 | tf_op jit(solution)/shard_map/ppermute | solution.py:430
  45.6 3.5 %collective-permute-done.4.refs_5_ = bf16[10,64,128]{2,1,0:T(8,128)(2,1)S(1)} collective-permute-done((bf16[10,64,128]{2,1,0:T(8,128)(2,1)S(1)}, bf16[10,64,128]{2,1,0:T(8,128)(2,1)S(1)}, u32[]{:S(2)}, u32[]{:S(2)}) %collective-permute-start.4) | collective-permute-done | bytes 163872 | tf_op jit(solution)/shard_map/ppermute | solution.py:430
  49.1 2.2 %collective-permute-done.2.refs_3_ = bf16[10,64,128]{2,1,0:T(8,128)(2,1)S(1)} collective-permute-done((bf16[10,64,128]{2,1,0:T(8,128)(2,1)S(1)}, bf16[10,64,128]{2,1,0:T(8,128)(2,1)S(1)}, u32[]{:S(2)}, u32[]{:S(2)}) %collective-permute-start.2) | collective-permute-done | bytes 163872 | tf_op jit(solution)/shard_map/ppermute | solution.py:430
  51.3 1.8 %collective-permute-done.6.refs_7_ = bf16[10,64,128]{2,1,0:T(8,128)(2,1)S(1)} collective-permute-done((bf16[10,64,128]{2,1,0:T(8,128)(2,1)S(1)}, bf16[10,64,128]{2,1,0:T(8,128)(2,1)S(1)}, u32[]{:S(2)}, u32[]{:S(2)}) %collective-permute-start.6) | collective-permute-done | bytes 163872 | tf_op jit(solution)/shard_map/ppermute | solution.py:430
  53.1 3.9 %project.1 = (bf16[2,64,1024]{2,1,0:T(8,128)(2,1)S(1)}, bf16[2,64,1024]{2,1,0:T(8,128)(2,1)S(1)}) custom-call(bf16[10,64,128]{2,1,0:T(8,128)(2,1)S(1)} %get-tuple-element.70.refs_0_, bf16[10,64,128]{2,1,0:T(8,128)(2,1)S(1)} %collective-permute-done.refs_1_, bf16[10,64,128]{2,1,0:T(8,128)(2,1)S(1)} %collective-permute-done.1.refs_2_, ...), custom_call_target="tpu_custom_call" | custom-call | tf_op jit(solution)/shard_map/project/pallas_call | solution.py:433
  57.0 0.1 collective-permute-start.7
  57.1 1.5 %collective-permute-done.7 = bf16[2,64,1024]{2,1,0:T(8,128)(2,1)S(1)} collective-permute-done((bf16[2,64,1024]{2,1,0:T(8,128)(2,1)S(1)}, bf16[2,64,1024]{2,1,0:T(8,128)(2,1)S(1)}, u32[]{:S(2)}, u32[]{:S(2)}) %collective-permute-start.7) | collective-permute-done | bytes 262176 | tf_op jit(solution)/shard_map/ppermute | solution.py:454
  58.7 1.6 %collective-permute-start.8 = (bf16[1,64,1024]{2,1,0:T(8,128)(2,1)S(1)}, bf16[1,64,1024]{2,1,0:T(8,128)(2,1)S(1)}, u32[]{:S(2)}, u32[]{:S(2)}) collective-permute-start(bf16[1,64,1024]{2,1,0:T(8,128)(2,1)S(1)} %fusion.2), channel_id=1, source_target_pairs={{0,2},{1,3},{2,0},{3,1},{4,6},{5,7},{6,4},{7,5},{8,10},{9,11},{10,... | collective-permute-start | bytes 393224 | tf_op jit(solution)/shard_map/ppermute | solution.py:454
  60.3 4.0 %collective-permute-done.8 = bf16[1,64,1024]{2,1,0:T(8,128)(2,1)S(1)} collective-permute-done((bf16[1,64,1024]{2,1,0:T(8,128)(2,1)S(1)}, bf16[1,64,1024]{2,1,0:T(8,128)(2,1)S(1)}, u32[]{:S(2)}, u32[]{:S(2)}) %collective-permute-start.8) | collective-permute-done | bytes 131104 | tf_op jit(solution)/shard_map/ppermute | solution.py:454
  64.4 0.7 %reshape.45 = bf16[16,4,1024]{2,1,0:T(4,128)(2,1)} reshape(bf16[1,64,1024]{2,1,0:T(8,128)(2,1)S(1)} %fusion.1) | data formatting | bytes 262144 | tf_op jit(solution)/shard_map/reshape | solution.py:461
  (11 shorter events, 0.1 us)
Async XLA Ops:
  2.0 14.8 %all-to-all-start.1 = ((bf16[8,80,128]{2,1,0:T(8,128)(2,1)}), bf16[8,80,128]{2,1,0:T(8,128)(2,1)S(1)}, u32[]{:S(2)}, u32[]{:S(2)}) async-start(bf16[8,80,128]{2,1,0:T(8,128)(2,1)} %ask.2), calls=%async_computation.1 | async-start | bytes 327680 | tf_op jit(solution)/shard_map/all_to_all | solution.py:362
  9.2 7.6 %copy-start.1 = (s32[64]{0:T(128)S(1)}, s32[64]{0:T(128)}, u32[]{:S(2)}) copy-start(s32[64]{0:T(128)} %slot_ref.5) | copy-start | bytes 772
  9.3 7.6 %copy-start.2 = (s32[64]{0:T(128)S(1)}, s32[64]{0:T(128)}, u32[]{:S(2)}) copy-start(s32[64]{0:T(128)} %len_ref.5) | copy-start | bytes 772
  16.8 2.8 %copy-start = (bf16[8,4,16,128]{3,2,1,0:T(8,128)(2,1)S(1)}, bf16[8,4,16,128]{3,2,1,0:T(8,128)(2,1)}, u32[]{:S(2)}) copy-start(bf16[8,4,16,128]{3,2,1,0:T(8,128)(2,1)} %param.10) | copy-start | bytes 393220
  20.3 13.2 %collective-permute-start.3 = (bf16[10,64,128]{2,1,0:T(8,128)(2,1)S(1)}, bf16[10,64,128]{2,1,0:T(8,128)(2,1)S(1)}, u32[]{:S(2)}, u32[]{:S(2)}) collective-permute-start(bf16[10,64,128]{2,1,0:T(8,128)(2,1)S(1)} %get-tuple-element.70.refs_0_), channel_id=1, source_target_pairs={{0,16},{4,20},{8,24},{12,28},{16,0},{20,4},{24,8},{28,12},{1,17},{... | collective-permute-start | bytes 491528 | tf_op jit(solution)/shard_map/ppermute | solution.py:430
  28.1 12.4 %collective-permute-start.1 = (bf16[10,64,128]{2,1,0:T(8,128)(2,1)S(1)}, bf16[10,64,128]{2,1,0:T(8,128)(2,1)S(1)}, u32[]{:S(2)}, u32[]{:S(2)}) collective-permute-start(bf16[10,64,128]{2,1,0:T(8,128)(2,1)S(1)} %get-tuple-element.70.refs_0_), channel_id=1, source_target_pairs={{0,8},{4,12},{8,0},{12,4},{16,24},{20,28},{24,16},{28,20},{1,9},{5... | collective-permute-start | bytes 491528 | tf_op jit(solution)/shard_map/ppermute | solution.py:430
  33.5 8.3 %collective-permute-start.5 = (bf16[10,64,128]{2,1,0:T(8,128)(2,1)S(1)}, bf16[10,64,128]{2,1,0:T(8,128)(2,1)S(1)}, u32[]{:S(2)}, u32[]{:S(2)}) collective-permute-start(bf16[10,64,128]{2,1,0:T(8,128)(2,1)S(1)} %collective-permute-done.3.refs_4_), channel_id=1, source_target_pairs={{0,8},{4,12},{8,0},{12,4},{16,24},{20,28},{24,16},{28,20},{1,9},{5... | collective-permute-start | bytes 491528 | tf_op jit(solution)/shard_map/ppermute | solution.py:430
  38.5 7.1 %collective-permute-start = (bf16[10,64,128]{2,1,0:T(8,128)(2,1)S(1)}, bf16[10,64,128]{2,1,0:T(8,128)(2,1)S(1)}, u32[]{:S(2)}, u32[]{:S(2)}) collective-permute-start(bf16[10,64,128]{2,1,0:T(8,128)(2,1)S(1)} %get-tuple-element.70.refs_0_), channel_id=1, source_target_pairs={{0,4},{4,0},{8,12},{12,8},{16,20},{20,16},{24,28},{28,24},{1,5},{5... | collective-permute-start | bytes 491528 | tf_op jit(solution)/shard_map/ppermute | solution.py:430
  39.0 10.1 %collective-permute-start.4 = (bf16[10,64,128]{2,1,0:T(8,128)(2,1)S(1)}, bf16[10,64,128]{2,1,0:T(8,128)(2,1)S(1)}, u32[]{:S(2)}, u32[]{:S(2)}) collective-permute-start(bf16[10,64,128]{2,1,0:T(8,128)(2,1)S(1)} %collective-permute-done.3.refs_4_), channel_id=1, source_target_pairs={{0,4},{4,0},{8,12},{12,8},{16,20},{20,16},{24,28},{28,24},{1,5},{5... | collective-permute-start | bytes 491528 | tf_op jit(solution)/shard_map/ppermute | solution.py:430
  40.6 10.8 %collective-permute-start.2 = (bf16[10,64,128]{2,1,0:T(8,128)(2,1)S(1)}, bf16[10,64,128]{2,1,0:T(8,128)(2,1)S(1)}, u32[]{:S(2)}, u32[]{:S(2)}) collective-permute-start(bf16[10,64,128]{2,1,0:T(8,128)(2,1)S(1)} %collective-permute-done.1.refs_2_), channel_id=1, source_target_pairs={{0,4},{4,0},{8,12},{12,8},{16,20},{20,16},{24,28},{28,24},{1,5},{5... | collective-permute-start | bytes 491528 | tf_op jit(solution)/shard_map/ppermute | solution.py:430
  41.8 11.3 %collective-permute-start.6 = (bf16[10,64,128]{2,1,0:T(8,128)(2,1)S(1)}, bf16[10,64,128]{2,1,0:T(8,128)(2,1)S(1)}, u32[]{:S(2)}, u32[]{:S(2)}) collective-permute-start(bf16[10,64,128]{2,1,0:T(8,128)(2,1)S(1)} %collective-permute-done.5.refs_6_), channel_id=1, source_target_pairs={{0,4},{4,0},{8,12},{12,8},{16,20},{20,16},{24,28},{28,24},{1,5},{5... | collective-permute-start | bytes 491528 | tf_op jit(solution)/shard_map/ppermute | solution.py:430
  57.0 1.6 %collective-permute-start.7 = (bf16[2,64,1024]{2,1,0:T(8,128)(2,1)S(1)}, bf16[2,64,1024]{2,1,0:T(8,128)(2,1)S(1)}, u32[]{:S(2)}, u32[]{:S(2)}) collective-permute-start(bf16[2,64,1024]{2,1,0:T(8,128)(2,1)S(1)} %get-tuple-element.72), channel_id=1, source_target_pairs={{0,1},{1,0},{2,3},{3,2},{4,5},{5,4},{6,7},{7,6},{8,9},{9,8},{10,11... | collective-permute-start | bytes 786440 | tf_op jit(solution)/shard_map/ppermute | solution.py:454
  58.7 5.6 %collective-permute-start.8 = (bf16[1,64,1024]{2,1,0:T(8,128)(2,1)S(1)}, bf16[1,64,1024]{2,1,0:T(8,128)(2,1)S(1)}, u32[]{:S(2)}, u32[]{:S(2)}) collective-permute-start(bf16[1,64,1024]{2,1,0:T(8,128)(2,1)S(1)} %fusion.2), channel_id=1, source_target_pairs={{0,2},{1,3},{2,0},{3,1},{4,6},{5,7},{6,4},{7,5},{8,10},{9,11},{10,... | collective-permute-start | bytes 393224 | tf_op jit(solution)/shard_map/ppermute | solution.py:454
